TPU v7x, 32 devices: a whole 2x2x4 slice. The times are simulated.
32 devices in a mesh: groups: 2 (over y), kvb: 4 (over z), tp: 4 (over x, core).
Axes of the slice: x: 2, y: 2, z: 4, core: 2. Of those that a mesh axis runs over, the one named last changes fastest.
Arguments:
- residual: bfloat16 [32, 8192], P(('groups', 'kvb')), parts along dimension 0, may hold values from -3 to 3
- queries: bfloat16 [32, 8192], P(('groups', 'kvb'), 'tp'), parts along dimension 0, may hold values from -60 to 60
- new_kv: bfloat16 [32, 2048], P(('groups', 'kvb')), parts along dimension 0, may hold values from -6 to 6
- kv_cache: bfloat16 [2048, 16, 2048], P(('groups', 'kvb', 'tp')), parts along dimension 0, may hold values from -6 to 6
- lengths: int32 [32], P('groups'), parts along dimension 0, may hold values from 1 to 2048, as said below
- slot_seq: int32 [2048], P(('groups', 'kvb', 'tp')), parts along dimension 0, may hold values from 0 to 15, as said below
- slot_block: int32 [2048], P(('groups', 'kvb', 'tp')), parts along dimension 0, may hold values from 0 to 127, as said below
- block_counts: int32 [32], P(('groups', 'kvb', 'tp')), parts along dimension 0, may hold values from 16 to 64, as said below
- out_weight: bfloat16 [8192, 8192], P('tp'), may hold values from -0.5 to 0.5
- norm_gain: bfloat16 [8192], P('tp'), may hold values from 0.099609375 to 1.8984375
Outputs:
- stream: bfloat16 [32, 8192], P(('groups', 'kvb'), 'tp'), parts along dimension 0
- normed: bfloat16 [32, 8192], P(('groups', 'kvb'), 'tp'), parts along dimension 0
There are 2 independent parts, one for each index of `groups`. A program takes and returns all parts, laid end to end along the dimension named above; an argument that names none is the same for every part. Nothing has to cross between parts.
Inputs may be any that keep to these rules, and one draw needn't show every extreme that they name: `block_counts`: slots below a device's count hold cache blocks, those at or beyond it none; at least one device's count is 64. `slot_seq`: each pair of a sequence s and a block b below ceil(lengths[s] / 16) sits in exactly one live slot of the group. `slot_block`: some sequence has exactly 128 blocks; none has more. `lengths`: some sequence has exactly 16 * (128) tokens.
All inputs are finite; a program needn't handle non-finite values.
Results may differ from a plain program's by a relative error of at most 0.006.
Values may be sent and summed in bfloat16 or wider, within the bound.
A program may use at most 64 MiB of HBM per device.

v0:
```python
import jax
import jax.numpy as jnp
from jax import lax
from jax.sharding import PartitionSpec as P

QH = 64
KVH = 8
HD = 128
BLK = 16


NEGATIVE = -1e30
EPSILON = 1e-06


def on_device(
    residual,
    queries,
    new_kv,
    kv_cache,
    lengths,
    slot_seq,
    slot_block,
    block_counts,
    out_weight,
    norm_gain,
):
    tp_count = lax.axis_size("tp")
    kvb_count = lax.axis_size("kvb")
    tp_index = lax.axis_index("tp")
    seq_rep = residual.shape[0]
    local_heads = queries.shape[1] // HD
    group_size = QH // KVH
    score_scale = HD ** (-0.5)
    wide = lax.all_gather(queries, "tp", axis=1, tiled=True)
    every = lax.all_gather(wide, "kvb", axis=0, tiled=True)
    seq_total = every.shape[0]
    grouped = every.reshape(seq_total, KVH, group_size, HD)
    pool_size = kv_cache.shape[0]
    step_slots = min(32, pool_size)
    live_count = block_counts[0]
    seq_ids = jnp.arange(seq_total, dtype=jnp.int32)
    offsets = jnp.arange(BLK, dtype=jnp.int32)

    def advance(turn_index, carried):
        peak_now, weight_sum, partial_rows = carried
        first_slot = turn_index * step_slots
        cache_part = lax.dynamic_slice_in_dim(kv_cache, first_slot, step_slots, 0)
        seq_part = lax.dynamic_slice_in_dim(slot_seq, first_slot, step_slots, 0)
        block_part = lax.dynamic_slice_in_dim(slot_block, first_slot, step_slots, 0)
        key_rows = cache_part[:, :, : KVH * HD].reshape(step_slots * BLK, KVH, HD)
        value_rows = cache_part[:, :, KVH * HD :].reshape(step_slots * BLK, KVH, HD)
        token_seq = jnp.repeat(seq_part, BLK)
        position = (block_part[:, None] * BLK + offsets[None, :]).reshape(-1)
        slot_live = jnp.repeat(
            first_slot + jnp.arange(step_slots, dtype=jnp.int32) < live_count, BLK
        )
        member = token_seq[None, :] == seq_ids[:, None]
        length_of = jnp.sum(jnp.where(member, lengths[:, None], 0), axis=0)
        live = member & (position < length_of)[None, :] & slot_live[None, :]
        mask = live[:, None, None, :]
        scores = (
            jnp.einsum("sgqd,ngd->sgqn", grouped, key_rows, preferred_element_type=jnp.float32)
            * score_scale
        )
        peak_next = jnp.maximum(peak_now, jnp.max(jnp.where(mask, scores, NEGATIVE), axis=-1))
        weights = jnp.where(mask, jnp.exp(scores - peak_next[..., None]), 0.0)
        shrink = jnp.exp(peak_now - peak_next)
        weight_sum = weight_sum * shrink + jnp.sum(weights, axis=-1)
        partial_rows = partial_rows * shrink[..., None] + jnp.einsum(
            "sgqn,ngd->sgqd",
            weights.astype(jnp.bfloat16),
            value_rows,
            preferred_element_type=jnp.float32,
        )
        return (peak_next, weight_sum, partial_rows)

    start_state = (
        jnp.full((seq_total, KVH, group_size), NEGATIVE, jnp.float32),
        jnp.zeros((seq_total, KVH, group_size), jnp.float32),
        jnp.zeros((seq_total, KVH, group_size, HD), jnp.float32),
    )
    turn_count = (live_count + step_slots - 1) // step_slots
    peak_now, weight_sum, partial_rows = lax.fori_loop(0, turn_count, advance, start_state)
    row_out = partial_rows.reshape(kvb_count, seq_rep, tp_count, local_heads * HD).transpose(
        0, 2, 1, 3
    )
    peak_out = peak_now.reshape(kvb_count, seq_rep, tp_count, local_heads).transpose(0, 2, 1, 3)
    sum_out = weight_sum.reshape(kvb_count, seq_rep, tp_count, local_heads).transpose(0, 2, 1, 3)
    device_total = kvb_count * tp_count
    got_rows, got_peaks, got_sums = (
        lax.all_to_all(
            row_out.reshape(device_total, seq_rep, local_heads * HD),
            ("kvb", "tp"),
            split_axis=0,
            concat_axis=0,
            tiled=True,
        ),
        lax.all_to_all(
            peak_out.reshape(device_total, seq_rep, local_heads),
            ("kvb", "tp"),
            split_axis=0,
            concat_axis=0,
            tiled=True,
        ),
        lax.all_to_all(
            sum_out.reshape(device_total, seq_rep, local_heads),
            ("kvb", "tp"),
            split_axis=0,
            concat_axis=0,
            tiled=True,
        ),
    )
    got_rows = got_rows.reshape(device_total, seq_rep, local_heads, HD)
    kv_local = max(1, local_heads // group_size)
    per_kv = local_heads // kv_local
    kv_first = tp_index * local_heads // group_size
    new_keys = lax.dynamic_slice_in_dim(new_kv, kv_first * HD, kv_local * HD, 1).reshape(
        seq_rep, kv_local, HD
    )
    new_values = lax.dynamic_slice_in_dim(new_kv, KVH * HD + kv_first * HD, kv_local * HD, 1)
    new_values = new_values.reshape(seq_rep, kv_local, 1, HD).astype(jnp.float32)
    own_view = queries.reshape(seq_rep, kv_local, per_kv, HD)
    fresh = (
        jnp.einsum("rkqd,rkd->rkq", own_view, new_keys, preferred_element_type=jnp.float32)
        * score_scale
    )
    fresh = fresh.reshape(seq_rep, local_heads)
    fresh_values = jnp.broadcast_to(new_values, (seq_rep, kv_local, per_kv, HD)).reshape(
        seq_rep, local_heads, HD
    )
    overall = jnp.maximum(jnp.max(got_peaks, axis=0), fresh)
    scaling = jnp.exp(got_peaks - overall[None])
    fresh_weight = jnp.exp(fresh - overall)
    denominator = jnp.sum(scaling * got_sums, axis=0) + fresh_weight
    numerator = (
        jnp.sum(scaling[..., None] * got_rows, axis=0) + fresh_weight[..., None] * fresh_values
    )
    attended = (
        (numerator / denominator[..., None]).reshape(seq_rep, local_heads * HD).astype(jnp.bfloat16)
    )
    projected = jnp.dot(attended, out_weight, preferred_element_type=jnp.float32)
    width_dev = norm_gain.shape[0]
    column = tp_index * width_dev
    summed = lax.psum(projected, "tp")
    full_stream = (residual.astype(jnp.float32) + summed).astype(jnp.bfloat16)
    full_wide = lax.optimization_barrier(full_stream).astype(jnp.float32)
    mean_square = jnp.mean(full_wide * full_wide, axis=1)
    stream = lax.dynamic_slice_in_dim(full_stream, column, width_dev, 1)
    stream_wide = lax.dynamic_slice_in_dim(full_wide, column, width_dev, 1)
    normed = (
        stream_wide * lax.rsqrt(mean_square + EPSILON)[:, None] * norm_gain.astype(jnp.float32)
    ).astype(jnp.bfloat16)
    return (stream, normed)


def solution(mesh):
    placed = (
        P(("groups", "kvb"), None),
        P(("groups", "kvb"), "tp"),
        P(("groups", "kvb"), None),
        P(("groups", "kvb", "tp"), None, None),
        P("groups"),
        P(("groups", "kvb", "tp")),
        P(("groups", "kvb", "tp")),
        P(("groups", "kvb", "tp")),
        P("tp", None),
        P("tp"),
    )
    return jax.shard_map(
        on_device,
        mesh=mesh,
        in_specs=placed,
        out_specs=(P(("groups", "kvb"), "tp"), P(("groups", "kvb"), "tp")),
        check_vma=False,
    )
```

profile of v0, /device:TPU:0, one launch (start us, length us, event | category | flops | bytes accessed | tf_op | source)
XLA Modules:
  0.0 140.4 jit_solution(4578274907591061050)
XLA Ops:
  7.8 6.5 %all_gather.6 = bf16[4,8192]{1,0:T(4,128)(2,1)S(1)} all-gather(bf16[4,2048]{1,0:T(4,128)(2,1)} %param.13), channel_id=1, replica_groups=mesh['groups'=2,'kvb'=4,'tp'=4] {'tp'}, dimensions={1}, use_global_device_ids=true | all-gather | bytes 81920 | tf_op jit(solution)/shard_map/all_gather | solution.py:35
  14.3 14.5 %all-gather = bf16[4,4,8192]{2,1,0:T(4,128)(2,1)S(1)} all-gather(bf16[1,4,8192]{2,1,0:T(4,128)(2,1)S(1)} %bitcast.100), channel_id=1, replica_groups=mesh['groups'=2,'kvb'=4,'tp'=4] {'kvb'}, dimensions={0}, use_global_device_ids=true | all-gather | bytes 327680 | tf_op jit(solution)/shard_map/all_gather | solution.py:36
  28.8 0.3 reshape.180
  29.1 0.2 copy.33
  29.4 7.9 %while.17 = (s32[]{:T(128)}, f32[16,8,8]{0,2,1:T(8,128)S(1)}, f32[16,8,8]{0,2,1:T(8,128)S(1)}, f32[16,8,8,128]{3,0,2,1:T(8,128)S(1)}, s32[]{:T(128)}, /*index=5*...) while((s32[]{:T(128)}, f32[16,8,8]{0,2,1:T(8,128)S(1)}, ...), condition=%wide.region_4.5_spmd.clone.clone, body=%wide.region_0.4_spmd.clone.clone.sunk | while | flops 274516576 | bytes 18212968 | solution.py:84
  29.4 0.7 dynamic_slice.42
  30.2 0.1 eq.54
  30.3 0.7 fusion.44
  31.1 0.7 dynamic-slice_multiply_fusion.2
  31.8 0.1 iota_add_fusion.2
  31.9 0.1 add.156
  32.0 0.7 add_compare_fusion.2
  32.6 0.1 broadcast_in_dim.135
  32.7 0.1 and.71
  32.8 1.7 %constant_dynamic-slice_fusion.5 = (bf16[32,16,1024]{2,1,0:T(8,128)(2,1)S(1)}, bf16[32,16,1024]{2,1,0:T(8,128)(2,1)S(1)}) fusion(bf16[64,16,2048]{2,1,0:T(8,128)(2,1)} %get-tuple-element.348, s32[]{:T(128)S(6)} %select_n.72, s32[]{:T(128)S(6)} %add.157), kind=kLoop, calls=%fused_computation.28.clone.1 | loop fusion | bytes 4194312 | tf_op jit(solution)/shard_map/while/body/slice | solution.py:52
  34.5 0.3 copy.84
  34.8 0.6 fusion.46
  35.4 0.6 fusion.47
  36.1 0.3 copy.85
  36.3 0.9 fusion.48
  37.3 0.1 copy.34
  37.4 0.1 reshape.181
  37.5 0.6 copy.36
  38.1 14.2 %all-to-all-start = ((f32[16,4,16]{2,1,0:T(4,128)}), f32[16,4,16]{2,1,0:T(4,128)S(1)}, u32[]{:S(2)}, u32[]{:S(2)}) async-start(f32[16,4,16]{2,1,0:T(4,128)} %copy.36), calls=%async_computation | async-start | bytes 65536 | tf_op jit(solution)/shard_map/all_to_all | solution.py:99
  52.3 0.7 dynamic-slice_convert_fusion
  53.0 0.1 copy.39
  53.1 0.1 reshape.189
  53.2 0.6 copy.41
  53.8 5.1 %all-to-all-done = f32[16,4,16]{2,1,0:T(4,128)S(1)} async-done(((f32[16,4,16]{2,1,0:T(4,128)}), f32[16,4,16]{2,1,0:T(4,128)S(1)}, u32[]{:S(2)}, u32[]{:S(2)}) %all-to-all-start) | async-done | bytes 4128 | tf_op jit(solution)/shard_map/all_to_all | solution.py:99
  58.9 3.5 %all-to-all-start.2 = ((f32[16,4,16]{2,1,0:T(4,128)}), f32[16,4,16]{2,1,0:T(4,128)S(1)}, u32[]{:S(2)}, u32[]{:S(2)}) async-start(f32[16,4,16]{2,1,0:T(4,128)} %copy.41), calls=%async_computation.2 | async-start | bytes 65536 | tf_op jit(solution)/shard_map/all_to_all | solution.py:106
  62.4 0.1 fusion.26
  62.6 0.2 copy.37
  62.7 0.2 reshape.186
  62.9 1.1 copy.38
  64.1 5.0 %all-to-all-done.2 = f32[16,4,16]{2,1,0:T(4,128)S(1)} async-done(((f32[16,4,16]{2,1,0:T(4,128)}), f32[16,4,16]{2,1,0:T(4,128)S(1)}, u32[]{:S(2)}, u32[]{:S(2)}) %all-to-all-start.2) | async-done | bytes 4128 | tf_op jit(solution)/shard_map/all_to_all | solution.py:106
  69.0 3.6 %all-to-all-start.1 = ((f32[16,4,2048]{2,1,0:T(4,128)}), f32[16,4,2048]{2,1,0:T(4,128)S(1)}, u32[]{:S(2)}, u32[]{:S(2)}) async-start(f32[16,4,2048]{2,1,0:T(4,128)} %bitcast.7), calls=%async_computation.1 | async-start | bytes 1048576 | tf_op jit(solution)/shard_map/all_to_all | solution.py:92
  72.7 0.1 reshape.185
  72.8 0.2 mul.96
  73.0 0.2 mul.97
  73.2 0.1 broadcast_bitcast_fusion
  73.3 13.5 %all-to-all-done.1 = f32[16,4,2048]{2,1,0:T(4,128)S(1)} async-done(((f32[16,4,2048]{2,1,0:T(4,128)}), f32[16,4,2048]{2,1,0:T(4,128)S(1)}, u32[]{:S(2)}, u32[]{:S(2)}) %all-to-all-start.1) | async-done | bytes 524320 | tf_op jit(solution)/shard_map/all_to_all | solution.py:92
  86.8 0.1 multiply_reduce_fusion
  87.0 13.5 %fusion.24 = f32[4,8192]{1,0:T(4,128)} fusion(bf16[2048,8192]{1,0:T(8,128)(2,1)} %param.20, f32[1,4,16,128]{3,2,1,0:T(8,128)S(1)} %get-tuple-element.225, f32[4,2048]{1,0:T(4,128)S(1)} %multiply_reduce_fusion, f32[1,4,16,128]{3,2,1,0:T(8,128)S(1)} %broadcast_bitcast_fusion.1, f32[1,4,16,128]{3,2,1,0:T(8,128)S(1)} %get-tuple-element.226), kind=kOutput, calls=%fused_computation.41 | convolution fusion | flops 134250496 | bytes 33816576 | tf_op jit(solution)/shard_map/dot_general | solution.py:142
  100.6 30.5 %all-reduce.2.cloned.1.call-done = f32[4,8192]{1,0:T(4,128)} async-done(((f32[4,8192]{1,0:T(4,128)}), f32[4,8192]{1,0:T(4,128)}) %all-reduce.2.cloned.1.call-update) | async-done | bytes 131088 | tf_op jit(solution)/shard_map/psum | solution.py:145
  131.0 0.9 add_convert_fusion
  132.0 0.2 multiply_reduce_fusion.1
  132.2 0.6 constant_dynamic-slice_fusion.2
  132.8 0.7 multiply_convert_fusion
  (30 shorter events, 0.4 us)
Async XLA Ops:
  29.4 33.0 %copy-start.1 = (bf16[4,2048]{1,0:T(4,128)(2,1)S(1)}, bf16[4,2048]{1,0:T(4,128)(2,1)}, u32[]{:S(2)}) copy-start(bf16[4,2048]{1,0:T(4,128)(2,1)} %param.13) | copy-start | bytes 49156
  38.1 20.8 %all-to-all-start = ((f32[16,4,16]{2,1,0:T(4,128)}), f32[16,4,16]{2,1,0:T(4,128)S(1)}, u32[]{:S(2)}, u32[]{:S(2)}) async-start(f32[16,4,16]{2,1,0:T(4,128)} %copy.36), calls=%async_computation | async-start | bytes 65536 | tf_op jit(solution)/shard_map/all_to_all | solution.py:99
  58.9 10.1 %all-to-all-start.2 = ((f32[16,4,16]{2,1,0:T(4,128)}), f32[16,4,16]{2,1,0:T(4,128)S(1)}, u32[]{:S(2)}, u32[]{:S(2)}) async-start(f32[16,4,16]{2,1,0:T(4,128)} %copy.41), calls=%async_computation.2 | async-start | bytes 65536 | tf_op jit(solution)/shard_map/all_to_all | solution.py:106
  69.0 17.8 %all-to-all-start.1 = ((f32[16,4,2048]{2,1,0:T(4,128)}), f32[16,4,2048]{2,1,0:T(4,128)S(1)}, u32[]{:S(2)}, u32[]{:S(2)}) async-start(f32[16,4,2048]{2,1,0:T(4,128)} %bitcast.7), calls=%async_computation.1 | async-start | bytes 1048576 | tf_op jit(solution)/shard_map/all_to_all | solution.py:92
  72.6 58.4 %all-reduce.2.cloned.1.call-start = ((), (), s32[]{:S(2)}) async-start(), calls=%async_computation.3 | async-start | bytes 262144 | tf_op jit(solution)/shard_map/psum | solution.py:145
  87.0 13.6 %copy-start.2 = (bf16[2048]{0:T(1024)(128)(2,1)S(1)}, bf16[2048]{0:T(1024)(128)(2,1)}, u32[]{:S(2)}) copy-start(bf16[2048]{0:T(1024)(128)(2,1)} %param.21) | copy-start | bytes 12292
  87.0 44.1 %copy-start = (bf16[4,8192]{1,0:T(4,128)(2,1)S(1)}, bf16[4,8192]{1,0:T(4,128)(2,1)}, u32[]{:S(2)}) copy-start(bf16[4,8192]{1,0:T(4,128)(2,1)} %param.12) | copy-start | bytes 196612
Sparse Core Ops, SparseCore 0:
  100.7 30.3 all-reduce.1
where the time goes:
time: 140 us
  waiting for transfers between devices  54 us (39%)
  starting transfers between devices  21.3 us (15%)
  blocking collectives  21 us (15%)
  matrix products  15.1 us (11%)
  between operations  14.9 us (11%)
  local copies, waits for them, and re-layouts  8.16 us (6%)
  other arithmetic  5.66 us (4%)
    psum x1, waiting for transfers between devices, on_device(): summed = lax.psum(projected, 'tp')  30.5 us
    all_gather x1, blocking collectives, on_device(): every = lax.all_gather(wide, 'kvb', axis=0, tiled=True)  14.5 us
    all_to_all x1, starting transfers between devices, on_device(): lax.all_to_all(peak_out.reshape(device_total, seq_rep, local_heads), ('kv...  14.2 us
    dot_general x1, matrix products, on_device(): jnp.dot(attended, out_weight, preferred_element_type=jnp.float32)  13.5 us
    all_to_all x1, waiting for transfers between devices, on_device(): lax.all_to_all(row_out.reshape(device_total, seq_rep, local_heads * HD),...  13.5 us
    all_gather x1, blocking collectives, on_device(): wide = lax.all_gather(queries, 'tp', axis=1, tiled=True)  6.46 us
    all_to_all x1, waiting for transfers between devices, on_device(): lax.all_to_all(peak_out.reshape(device_total, seq_rep, local_heads), ('kv...  5.08 us
    all_to_all x1, waiting for transfers between devices, on_device(): lax.all_to_all(sum_out.reshape(device_total, seq_rep, local_heads), ('kvb...  4.97 us
  transfers between devices with their start and end apart: 4, of which 4 were waited for; matrix products, arithmetic and copies ran while one was open for 3% of the time, Pallas kernels for 0%

commit v1 on v0

v1 whole, which is shorter than its diff:
```python
import math

import jax
import jax.numpy as jnp
from jax import lax
from jax.experimental import pallas as pl
from jax.experimental.pallas import tpu as pltpu
from jax.sharding import PartitionSpec as P

QH = 64
KVH = 8
HD = 128
BLK = 16
GROUP_HEADS = QH // KVH

NEGATIVE = -1e30
EPSILON = 1e-06
LANES = 128
TOKEN_LOG2 = math.log2(math.e) * HD ** (-0.5)
MESH = pl.DeviceIdType.MESH


def kernel(
    nz,
    nt,
    seq_rep,
    local_heads,
    lengths_ref,
    counts_ref,
    slot_seq_ref,
    slot_block_ref,
    residual_ref,
    queries_ref,
    new_kv_ref,
    gain_ref,
    cache_ref,
    weight_ref,
    stream_ref,
    normed_ref,
    cache_buf,
    weight_buf,
    bias_buf,
    row_buf,
    new_buf,
    q_all,
    part_tp,
    stat_tp,
    part_send,
    stat_send,
    z_send,
    z_stat_send,
    z_part,
    z_stat,
    lhs_buf,
    proj_send,
    proj_recv,
    ss_send,
    ss_recv,
    cache_sem,
    weight_sem,
    qz_send,
    qz_recv,
    qt_send,
    qt_recv,
    pt_send,
    pt_recv,
    st_send,
    st_recv,
    zp_send,
    zp_recv,
    zs_send,
    zs_recv,
    rs_send,
    rs_recv,
    sq_send,
    sq_recv,
):
    z = lax.axis_index("kvb")
    t = lax.axis_index("tp")
    kv_local = max(1, local_heads // GROUP_HEADS)
    per_kv = local_heads // kv_local
    sub = per_kv * seq_rep
    rows = nz * sub
    tokens = cache_buf.shape[0]
    slots = slot_seq_ref.shape[1]
    width = gain_ref.shape[1]
    fast = 2 if nt % 2 == 0 else 1
    slow = nt // fast

    def tp_to(j):
        return lax.rem(t // fast + j // fast, slow) * fast + lax.rem(t % fast + j % fast, fast)

    def tp_from(j):
        back = (slow - j // fast) % slow
        back_fast = (fast - j % fast) % fast
        return lax.rem(t // fast + back, slow) * fast + lax.rem(t % fast + back_fast, fast)

    def z_to(a):
        return lax.rem(z + a, nz)

    def z_back(a):
        return lax.rem(z + (nz - a), nz)

    far_first = sorted(range(1, nt), key=lambda j: (j < fast, j))

    cache_copy = pltpu.make_async_copy(cache_ref, cache_buf, cache_sem)
    cache_copy.start()
    weight_copies = {}
    for j in far_first + [0]:
        columns = pl.ds(pl.multiple_of(tp_to(j) * width, LANES), width)
        weight_copies[j] = pltpu.make_async_copy(
            weight_ref.at[:, columns], weight_buf.at[j], weight_sem.at[j]
        )
        weight_copies[j].start()

    barrier = pltpu.get_barrier_semaphore()
    for a in range(1, nz):
        pl.semaphore_signal(barrier, inc=1, device_id={"kvb": z_to(a)}, device_id_type=MESH)
    for j in range(1, nt):
        pl.semaphore_signal(barrier, inc=1, device_id={"tp": tp_to(j)}, device_id_type=MESH)

    wide_q = queries_ref[...].astype(jnp.float32)
    for k in range(kv_local):
        for q in range(per_kv):
            head = k * per_kv + q
            row_buf[k, q * seq_rep : (q + 1) * seq_rep, :] = wide_q[:, head * HD : (head + 1) * HD]
    for k in range(kv_local):
        q_all[0, 0, k] = row_buf[k].astype(jnp.bfloat16)
    pl.semaphore_wait(barrier, nz - 1 + nt - 1)

    pending = []

    def remote(src, dst, send, recv, target):
        copy = pltpu.make_async_remote_copy(
            src_ref=src,
            dst_ref=dst,
            send_sem=send,
            recv_sem=recv,
            device_id=target,
            device_id_type=MESH,
        )
        copy.start()
        pending.append(copy)
        return copy

    z_order = sorted(range(1, nz), key=lambda a: min(a, nz - a))
    q_from_z = {}
    for a in reversed(z_order):
        q_from_z[a] = remote(
            q_all.at[0, 0], q_all.at[0, a], qz_send.at[a], qz_recv.at[a], {"kvb": z_to(a)}
        )
    q_from_tp = {}

    def forward(a):
        for j in far_first:
            q_from_tp[a, j] = remote(
                q_all.at[0, a],
                q_all.at[j, a],
                qt_send.at[a, j],
                qt_recv.at[a, j],
                {"tp": tp_to(j)},
            )

    forward(0)

    row_id = lax.broadcasted_iota(jnp.int32, (rows, slots), 0)
    slot_id = lax.broadcasted_iota(jnp.int32, (rows, slots), 1)
    row_seq = lax.rem(z + nz - row_id // sub, nz) * seq_rep + lax.rem(row_id, seq_rep)
    row_len = jnp.zeros((rows, slots), jnp.int32)
    for s in range(nz * seq_rep):
        row_len = jnp.where(row_seq == s, lengths_ref[s], row_len)
    held = (row_seq == slot_seq_ref[...]) & (slot_id < counts_ref[0])
    limit = jnp.where(held, jnp.clip(row_len - BLK * slot_block_ref[...], 0, BLK), 0)
    token_slot = lax.broadcasted_iota(jnp.int32, (slots, tokens), 1) // BLK
    spread = (token_slot == lax.broadcasted_iota(jnp.int32, (slots, tokens), 0)).astype(jnp.float32)
    reach = jnp.dot(
        limit.astype(jnp.float32).astype(jnp.bfloat16),
        spread.astype(jnp.bfloat16),
        preferred_element_type=jnp.float32,
    )
    offset = lax.rem(lax.broadcasted_iota(jnp.int32, (rows, tokens), 1), BLK).astype(jnp.float32)
    bias_buf[...] = jnp.where(offset < reach, 0.0, NEGATIVE)

    own_kv = t * local_heads // GROUP_HEADS
    fresh = []
    for k in range(kv_local):
        for part in range(2):
            at = pl.multiple_of((part * KVH + own_kv + k) * HD, LANES)
            piece = new_kv_ref[:, pl.ds(at, HD)].astype(jnp.float32)
            for q in range(per_kv):
                new_buf[k, part, q * seq_rep : (q + 1) * seq_rep, :] = piece
        fresh.append(jnp.sum(row_buf[k] * new_buf[k, 0], axis=1, keepdims=True) * TOKEN_LOG2)
    lhs_buf[...] = jnp.zeros_like(lhs_buf)

    for a in z_order:
        q_from_z[a].wait_recv()
        forward(a)

    cache_copy.wait()
    lane = lax.broadcasted_iota(jnp.int32, (rows, LANES), 1)
    parts, stats = {}, {}
    for j in range(nt):
        if j > 0:
            for a in range(nz):
                q_from_tp[a, j].wait_recv()
        first_kv = tp_from(j) * local_heads // GROUP_HEADS
        for k in range(kv_local):
            key_at = pl.multiple_of((first_kv + k) * HD, LANES)
            value_at = pl.multiple_of((KVH + first_kv + k) * HD, LANES)
            q_rows = q_all[j, :, k].reshape(rows, HD)
            scores = lax.dot_general(
                q_rows,
                cache_buf[:, pl.ds(key_at, HD)],
                (((1,), (1,)), ((), ())),
                preferred_element_type=jnp.float32,
            )
            scores = scores * TOKEN_LOG2 + bias_buf[...]
            peak = jnp.max(scores, axis=1, keepdims=True)
            weights = jnp.exp2(scores - jnp.maximum(peak, 0.1 * NEGATIVE))
            total = jnp.sum(weights, axis=1, keepdims=True)
            partial = jnp.dot(
                weights.astype(jnp.bfloat16),
                cache_buf[:, pl.ds(value_at, HD)],
                preferred_element_type=jnp.float32,
            ).astype(jnp.bfloat16)
            tile = jnp.where(lane == 0, peak, total).T[:8]
            if j == 0:
                part_tp[0, k] = partial
                stat_tp[0, k] = tile
            else:
                part_send[j, k] = partial
                stat_send[j, k] = tile
        if j > 0:
            target = {"tp": tp_from(j)}
            stats[j] = remote(
                stat_send.at[j], stat_tp.at[j], st_send.at[j], st_recv.at[j], target
            )
            parts[j] = remote(
                part_send.at[j], part_tp.at[j], pt_send.at[j], pt_recv.at[j], target
            )

    for j in range(1, nt):
        stats[j].wait_recv()
        parts[j].wait_recv()

    def columns_of(pieces):
        height = -(-len(pieces) // 8) * 8
        index = lax.broadcasted_iota(jnp.int32, (height, rows), 0)
        tile = jnp.zeros((height, rows), jnp.float32)
        for i, piece in enumerate(pieces):
            tile = jnp.where(index == i, piece, tile)
        return tile.T

    for k in range(kv_local):
        peaks = [stat_tp[j, k, 0:1, :] for j in range(nt)]
        top = peaks[0]
        for piece in peaks[1:]:
            top = jnp.maximum(top, piece)
        scale = [jnp.exp2(piece - top) for piece in peaks]
        total = scale[0] * stat_tp[0, k, 1:2, :]
        for j in range(1, nt):
            total += scale[j] * stat_tp[j, k, 1:2, :]
        spread_scale = columns_of(scale)
        joined = spread_scale[:, 0:1] * part_tp[0, k].astype(jnp.float32)
        for j in range(1, nt):
            joined += spread_scale[:, j : j + 1] * part_tp[j, k].astype(jnp.float32)
        joined = joined.astype(jnp.bfloat16)
        index = lax.broadcasted_iota(jnp.int32, (8, rows), 0)
        tile = jnp.where(index == 0, top, total)
        z_stat_send[k] = tile
        z_stat[0, k] = tile
        z_part[0, k] = joined[:sub]
        for a in range(1, nz):
            z_send[a, k] = joined[a * sub : (a + 1) * sub]
    from_z = {}
    for a in reversed(z_order):
        target = {"kvb": z_back(a)}
        from_z[a] = (
            remote(z_stat_send, z_stat.at[a], zs_send.at[a], zs_recv.at[a], target),
            remote(z_send.at[a], z_part.at[a], zp_send.at[a], zp_recv.at[a], target),
        )
    for a in z_order:
        for copy in from_z[a]:
            copy.wait_recv()

    for k in range(kv_local):
        spread_stat = columns_of([z_stat[a, k, i : i + 1, :] for a in range(nz) for i in range(2)])
        peaks = [spread_stat[a * sub : (a + 1) * sub, 2 * a : 2 * a + 1] for a in range(nz)]
        sums = [spread_stat[a * sub : (a + 1) * sub, 2 * a + 1 : 2 * a + 2] for a in range(nz)]
        top = fresh[k]
        for piece in peaks:
            top = jnp.maximum(top, piece)
        denominator = jnp.exp2(fresh[k] - top)
        numerator = denominator * new_buf[k, 1]
        for a in range(nz):
            scale = jnp.exp2(peaks[a] - top)
            denominator += scale * sums[a]
            numerator += scale * z_part[a, k].astype(jnp.float32)
        row_buf[k] = numerator / denominator
        for q in range(per_kv):
            head = k * per_kv + q
            lhs_buf[0:seq_rep, head * HD : (head + 1) * HD] = row_buf[
                k, q * seq_rep : (q + 1) * seq_rep, :
            ]
    attended = lhs_buf[...].astype(jnp.bfloat16)

    step = min(512, width)
    reduced = {}
    for j in far_first + [0]:
        weight_copies[j].wait()

        def column_step(i, carry, j=j):
            at = pl.ds(pl.multiple_of(i * step, LANES), step)
            got = jnp.dot(attended, weight_buf[j, :, at], preferred_element_type=jnp.float32)
            proj_send[j, :, at] = got[:seq_rep]
            return carry

        lax.fori_loop(0, width // step, column_step, 0)
        if j > 0:
            reduced[j] = remote(
                proj_send.at[j],
                proj_recv.at[j],
                rs_send.at[j],
                rs_recv.at[j],
                {"tp": tp_to(j)},
            )
    own = pl.ds(pl.multiple_of(t * width, LANES), width)
    summed = proj_send[0]
    for j in far_first:
        reduced[j].wait_recv()
        summed += proj_recv[j]
    stream = (residual_ref[:, own].astype(jnp.float32) + summed).astype(jnp.bfloat16)
    stream_ref[...] = stream
    stream_wide = stream.astype(jnp.float32)
    square = jnp.sum(stream_wide * stream_wide, axis=1, keepdims=True)
    ss_send[...] = jnp.broadcast_to(square, ss_send.shape)
    squares = [
        remote(ss_send, ss_recv.at[j], sq_send.at[j], sq_recv.at[j], {"tp": tp_to(j)})
        for j in far_first
    ]
    gain = gain_ref[...].astype(jnp.float32)
    for copy in squares:
        copy.wait_recv()
    for j in range(1, nt):
        square += ss_recv[j][:, 0:1]
    mean_square = square * (1.0 / (width * nt))
    normed_ref[...] = (stream_wide * lax.rsqrt(mean_square + EPSILON) * gain).astype(jnp.bfloat16)
    for copy in pending:
        copy.wait_send()


def on_device(
    residual,
    queries,
    new_kv,
    kv_cache,
    lengths,
    slot_seq,
    slot_block,
    block_counts,
    out_weight,
    norm_gain,
):
    nt = lax.axis_size("tp")
    nz = lax.axis_size("kvb")
    seq_rep = residual.shape[0]
    local_heads = queries.shape[1] // HD
    kv_local = max(1, local_heads // GROUP_HEADS)
    sub = local_heads // kv_local * seq_rep
    rows = nz * sub
    slots = kv_cache.shape[0]
    tokens = slots * BLK
    width = norm_gain.shape[0]
    depth = out_weight.shape[0]
    bf16, f32 = jnp.bfloat16, jnp.float32
    dma = pltpu.SemaphoreType.DMA
    vmem = pl.BlockSpec(memory_space=pltpu.VMEM)
    smem = pl.BlockSpec(memory_space=pltpu.SMEM)
    hbm = pl.BlockSpec(memory_space=pl.ANY)

    def body(*refs):
        kernel(nz, nt, seq_rep, local_heads, *refs)

    return pl.pallas_call(
        body,
        out_shape=(
            jax.ShapeDtypeStruct((seq_rep, width), bf16),
            jax.ShapeDtypeStruct((seq_rep, width), bf16),
        ),
        in_specs=[smem, smem, vmem, vmem, vmem, vmem, vmem, vmem, hbm, hbm],
        out_specs=(vmem, vmem),
        scratch_shapes=[
            pltpu.VMEM((tokens, kv_cache.shape[2]), bf16),
            pltpu.VMEM((nt, depth, width), bf16),
            pltpu.VMEM((rows, tokens), f32),
            pltpu.VMEM((kv_local, sub, HD), f32),
            pltpu.VMEM((kv_local, 2, sub, HD), f32),
            pltpu.VMEM((nt, nz, kv_local, sub, HD), bf16),
            pltpu.VMEM((nt, kv_local, rows, HD), bf16),
            pltpu.VMEM((nt, kv_local, 8, rows), f32),
            pltpu.VMEM((nt, kv_local, rows, HD), bf16),
            pltpu.VMEM((nt, kv_local, 8, rows), f32),
            pltpu.VMEM((nz, kv_local, sub, HD), bf16),
            pltpu.VMEM((kv_local, 8, rows), f32),
            pltpu.VMEM((nz, kv_local, sub, HD), bf16),
            pltpu.VMEM((nz, kv_local, 8, rows), f32),
            pltpu.VMEM((16, depth), f32),
            pltpu.VMEM((nt, seq_rep, width), f32),
            pltpu.VMEM((nt, seq_rep, width), f32),
            pltpu.VMEM((seq_rep, LANES), f32),
            pltpu.VMEM((nt, seq_rep, LANES), f32),
            dma,
            dma((nt,)),
            dma((nz,)),
            dma((nz,)),
            dma((nz, nt)),
            dma((nz, nt)),
            dma((nt,)),
            dma((nt,)),
            dma((nt,)),
            dma((nt,)),
            dma((nz,)),
            dma((nz,)),
            dma((nz,)),
            dma((nz,)),
            dma((nt,)),
            dma((nt,)),
            dma((nt,)),
            dma((nt,)),
        ],
        compiler_params=pltpu.CompilerParams(
            collective_id=0, has_side_effects=True, vmem_limit_bytes=62 * 1024 * 1024
        ),
    )(
        lengths,
        block_counts,
        slot_seq.reshape(1, slots),
        slot_block.reshape(1, slots),
        residual,
        queries,
        new_kv,
        norm_gain.reshape(1, width),
        kv_cache.reshape(tokens, kv_cache.shape[2]),
        out_weight,
    )


def solution(mesh):
    placed = (
        P(("groups", "kvb"), None),
        P(("groups", "kvb"), "tp"),
        P(("groups", "kvb"), None),
        P(("groups", "kvb", "tp"), None, None),
        P("groups"),
        P(("groups", "kvb", "tp")),
        P(("groups", "kvb", "tp")),
        P(("groups", "kvb", "tp")),
        P("tp", None),
        P("tp"),
    )
    return jax.shard_map(
        on_device,
        mesh=mesh,
        in_specs=placed,
        out_specs=(P(("groups", "kvb"), "tp"), P(("groups", "kvb"), "tp")),
        check_vma=False,
    )
```

time: 140 us -> 39.5 us (0.28)
  waiting for transfers between devices: 54 us -> 0 us
  Pallas kernels: 0 us -> 33.9 us
  starting transfers between devices: 21.3 us -> 0 us
  blocking collectives: 21 us -> 0 us
  matrix products: 15.1 us -> 0 us
  between operations: 14.9 us -> 1.29 us
  other arithmetic: 5.66 us -> 0 us
  local copies, waits for them, and re-layouts: 8.16 us -> 3.95 us
    pallas_call x0 -> x1, Pallas kernels: none -> 33.9 us  [on_device(): pl.pallas_call(body, out_shape=(jax.ShapeDtypeStruct((seq_rep, width), bf...]
    psum x1 -> x0, waiting for transfers between devices: 30.5 us -> none  [on_device(): summed = lax.psum(projected, 'tp')]
    all_to_all x3 -> x0, waiting for transfers between devices: 23.6 us -> none  [the longest x1 13.5 us: on_device(): lax.all_to_all(row_out.reshape(device_total, seq_rep, local_heads * HD),...]
    all_to_all x3 -> x0, starting transfers between devices: 21.2 us -> none  [the longest x1 14.2 us: on_device(): lax.all_to_all(peak_out.reshape(device_total, seq_rep, local_heads), ('kv...]
    all_gather x2 -> x0, blocking collectives: 21 us -> none  [the longest x1 14.5 us: on_device(): every = lax.all_gather(wide, 'kvb', axis=0, tiled=True)]
    dot_general x4 -> x0, matrix products: 15.1 us -> none  [the longest x1 13.5 us: on_device(): jnp.dot(attended, out_weight, preferred_element_type=jnp.float32)]
    unnamed x9 -> x2, local copies, waits for them, and re-layouts: 0.27 us -> 2.66 us
    convert_element_type x5 -> x0, other arithmetic: 2.35 us -> none  [the longest x1 0.94 us: on_device(): full_stream = (residual.astype(jnp.float32) + summed).astype(jnp.bfloat16)]
  transfers between devices with their start and end apart: 4 -> 0, of which waited for: 4 -> 0; matrix products, arithmetic and copies ran while one was open for 3% -> 0% of each run, Pallas kernels for 0% -> 0%
where the time goes in v1:
time: 39.5 us; the launch traced here: 39.1 us
  Pallas kernels  33.9 us (86%)
  local copies, waits for them, and re-layouts  3.95 us (10%)
  between operations  1.29 us (3%)
    pallas_call x1, Pallas kernels, on_device(): pl.pallas_call(body, out_shape=(jax.ShapeDtypeStruct((seq_rep, width), bf...  33.9 us
    unnamed x2, local copies, waits for them, and re-layouts  2.66 us
    reshape x1, local copies, waits for them, and re-layouts, on_device(): norm_gain.reshape(1, width)  1.29 us

profile of v1, /device:TPU:0, one launch (start us, length us, event | category | flops | bytes accessed | tf_op | source)
XLA Modules:
  0.0 39.1 jit_solution(15105730968181179656)
XLA Ops:
  1.3 1.3 %reshape.18.refs_7_ = bf16[1,2048]{1,0:T(2,128)(2,1)} reshape(bf16[2048]{0:T(1024)(128)(2,1)} %param.19) | data formatting | bytes 8192 | tf_op jit(solution)/shard_map/reshape | solution.py:442
  2.6 33.9 %shard_map.113 = (bf16[4,2048]{1,0:T(4,128)(2,1)}, bf16[4,2048]{1,0:T(4,128)(2,1)}) custom-call(s32[16]{0:T(128)} %refs_0_.1, s32[1]{0:T(128)S(6)} %copy.14.refs_1_, s32[1,64]{1,0:T(1,128)} %bitcast.4, s32[1,64]{1,0:T(1,128)} %bitcast.5, bf16[4,8192]{1,0:T(4,128)(2,1)} %refs_4_.1, bf16[4,2048]{1,0:T(4,128)(2,1)} %refs_5_.1, bf16[4,2048]{1,0:T(4,128)(2,1)} %refs_6_.1, ...), custom_call_target="tpu_custom_call" | custom-call | tf_op jit(solution)/shard_map/pallas_call | solution.py:384
  36.4 1.3 %copy.15 = bf16[4,2048]{1,0:T(4,128)(2,1)} copy(bf16[4,2048]{1,0:T(4,128)(2,1)} %get-tuple-element.4) | data formatting | bytes 32768
  37.8 1.3 %copy.16 = bf16[4,2048]{1,0:T(4,128)(2,1)} copy(bf16[4,2048]{1,0:T(4,128)(2,1)} %get-tuple-element.5) | data formatting | bytes 32768

commit v2 on v1

--- a/solution.py
+++ b/solution.py
@@ -27,16 +27,22 @@
     local_heads,
     lengths_ref,
     counts_ref,
+    slot_seq_hbm,
+    slot_block_hbm,
+    residual_hbm,
+    queries_hbm,
+    new_kv_hbm,
+    gain_hbm,
+    cache_ref,
+    weight_ref,
+    stream_ref,
+    factor_ref,
     slot_seq_ref,
     slot_block_ref,
     residual_ref,
     queries_ref,
     new_kv_ref,
     gain_ref,
-    cache_ref,
-    weight_ref,
-    stream_ref,
-    normed_ref,
     cache_buf,
     weight_buf,
     bias_buf,
@@ -56,6 +62,7 @@
     proj_recv,
     ss_send,
     ss_recv,
+    input_sem,
     cache_sem,
     weight_sem,
     qz_send,
@@ -83,7 +90,7 @@
     rows = nz * sub
     tokens = cache_buf.shape[0]
     slots = slot_seq_ref.shape[1]
-    width = gain_ref.shape[1]
+    width = stream_ref.shape[1]
     fast = 2 if nt % 2 == 0 else 1
     slow = nt // fast
 
@@ -102,16 +109,6 @@
         return lax.rem(z + (nz - a), nz)
 
     far_first = sorted(range(1, nt), key=lambda j: (j < fast, j))
-
-    cache_copy = pltpu.make_async_copy(cache_ref, cache_buf, cache_sem)
-    cache_copy.start()
-    weight_copies = {}
-    for j in far_first + [0]:
-        columns = pl.ds(pl.multiple_of(tp_to(j) * width, LANES), width)
-        weight_copies[j] = pltpu.make_async_copy(
-            weight_ref.at[:, columns], weight_buf.at[j], weight_sem.at[j]
-        )
-        weight_copies[j].start()
 
     barrier = pltpu.get_barrier_semaphore()
     for a in range(1, nz):
@@ -119,6 +116,26 @@
     for j in range(1, nt):
         pl.semaphore_signal(barrier, inc=1, device_id={"tp": tp_to(j)}, device_id_type=MESH)
 
+    own = pl.ds(pl.multiple_of(t * width, LANES), width)
+    inputs = [
+        pltpu.make_async_copy(src, dst, input_sem.at[i])
+        for i, (src, dst) in enumerate(
+            (
+                (queries_hbm, queries_ref),
+                (slot_seq_hbm, slot_seq_ref),
+                (slot_block_hbm, slot_block_ref),
+                (new_kv_hbm, new_kv_ref),
+                (residual_hbm.at[:, own], residual_ref),
+                (gain_hbm, gain_ref),
+            )
+        )
+    ]
+    for copy in inputs:
+        copy.start()
+    cache_copy = pltpu.make_async_copy(cache_ref, cache_buf, cache_sem)
+    cache_copy.start()
+    inputs[0].wait()
+
     wide_q = queries_ref[...].astype(jnp.float32)
     for k in range(kv_local):
         for q in range(per_kv):
@@ -126,7 +143,8 @@
             row_buf[k, q * seq_rep : (q + 1) * seq_rep, :] = wide_q[:, head * HD : (head + 1) * HD]
     for k in range(kv_local):
         q_all[0, 0, k] = row_buf[k].astype(jnp.bfloat16)
-    pl.semaphore_wait(barrier, nz - 1 + nt - 1)
+    with jax.named_scope("barrier_wait"):
+        pl.semaphore_wait(barrier, nz - 1 + nt - 1)
 
     pending = []
 
@@ -162,6 +180,20 @@
             )
 
     forward(0)
+
+    depth = weight_buf.shape[0] // kv_local
+    pieces = 4
+    weight_copies = []
+    for i in range(kv_local * pieces):
+        part_rows = pl.ds(i * (depth // pieces), depth // pieces)
+        weight_copies.append(
+            pltpu.make_async_copy(
+                weight_ref.at[part_rows, :], weight_buf.at[part_rows, :], weight_sem.at[i]
+            )
+        )
+        weight_copies[i].start()
+    for copy in inputs[1:]:
+        copy.wait()
 
     row_id = lax.broadcasted_iota(jnp.int32, (rows, slots), 0)
     slot_id = lax.broadcasted_iota(jnp.int32, (rows, slots), 1)
@@ -193,55 +225,71 @@
     lhs_buf[...] = jnp.zeros_like(lhs_buf)
 
     for a in z_order:
-        q_from_z[a].wait_recv()
+        with jax.named_scope(f"q_z_wait{a}"):
+            q_from_z[a].wait_recv()
         forward(a)
 
-    cache_copy.wait()
+    with jax.named_scope("cache_wait"):
+        cache_copy.wait()
     lane = lax.broadcasted_iota(jnp.int32, (rows, LANES), 1)
-    parts, stats = {}, {}
-    for j in range(nt):
-        if j > 0:
-            for a in range(nz):
-                q_from_tp[a, j].wait_recv()
+    copies = {}
+
+    def attend(j, k):
         first_kv = tp_from(j) * local_heads // GROUP_HEADS
-        for k in range(kv_local):
-            key_at = pl.multiple_of((first_kv + k) * HD, LANES)
-            value_at = pl.multiple_of((KVH + first_kv + k) * HD, LANES)
-            q_rows = q_all[j, :, k].reshape(rows, HD)
-            scores = lax.dot_general(
-                q_rows,
-                cache_buf[:, pl.ds(key_at, HD)],
-                (((1,), (1,)), ((), ())),
-                preferred_element_type=jnp.float32,
-            )
-            scores = scores * TOKEN_LOG2 + bias_buf[...]
-            peak = jnp.max(scores, axis=1, keepdims=True)
-            weights = jnp.exp2(scores - jnp.maximum(peak, 0.1 * NEGATIVE))
-            total = jnp.sum(weights, axis=1, keepdims=True)
-            partial = jnp.dot(
-                weights.astype(jnp.bfloat16),
-                cache_buf[:, pl.ds(value_at, HD)],
-                preferred_element_type=jnp.float32,
-            ).astype(jnp.bfloat16)
-            tile = jnp.where(lane == 0, peak, total).T[:8]
-            if j == 0:
-                part_tp[0, k] = partial
-                stat_tp[0, k] = tile
-            else:
-                part_send[j, k] = partial
-                stat_send[j, k] = tile
-        if j > 0:
-            target = {"tp": tp_from(j)}
-            stats[j] = remote(
-                stat_send.at[j], stat_tp.at[j], st_send.at[j], st_recv.at[j], target
-            )
-            parts[j] = remote(
-                part_send.at[j], part_tp.at[j], pt_send.at[j], pt_recv.at[j], target
-            )
-
-    for j in range(1, nt):
-        stats[j].wait_recv()
-        parts[j].wait_recv()
+        key_at = pl.multiple_of((first_kv + k) * HD, LANES)
+        value_at = pl.multiple_of((KVH + first_kv + k) * HD, LANES)
+        q_rows = q_all[j, :, k].reshape(rows, HD)
+        scores = lax.dot_general(
+            q_rows,
+            cache_buf[:, pl.ds(key_at, HD)],
+            (((1,), (1,)), ((), ())),
+            preferred_element_type=jnp.float32,
+        )
+        scores = scores * TOKEN_LOG2 + bias_buf[...]
+        peak = jnp.max(scores, axis=1, keepdims=True)
+        weights = jnp.exp2(scores - jnp.maximum(peak, 0.1 * NEGATIVE))
+        total = jnp.sum(weights, axis=1, keepdims=True)
+        partial = jnp.dot(
+            weights.astype(jnp.bfloat16),
+            cache_buf[:, pl.ds(value_at, HD)],
+            preferred_element_type=jnp.float32,
+        ).astype(jnp.bfloat16)
+        tile = jnp.where(lane == 0, peak, total).T[:8]
+        if j == 0:
+            part_tp[0, k] = partial
+            stat_tp[0, k] = tile
+            return
+        part_send[j, k] = partial
+        stat_send[j, k] = tile
+        target = {"tp": tp_from(j)}
+        copies[j, k] = (
+            remote(
+                stat_send.at[j, k],
+                stat_tp.at[j, k],
+                st_send.at[j, k],
+                st_recv.at[j, k],
+                target,
+            ),
+            remote(
+                part_send.at[j, k],
+                part_tp.at[j, k],
+                pt_send.at[j, k],
+                pt_recv.at[j, k],
+                target,
+            ),
+        )
+
+    for k in range(kv_local):
+        attend(0, k)
+    arrived = set()
+    for k in range(kv_local):
+        for j in far_first if k == kv_local - 1 else range(1, nt):
+            if j not in arrived:
+                arrived.add(j)
+                with jax.named_scope(f"q_tp_wait{j}"):
+                    for a in range(nz):
+                        q_from_tp[a, j].wait_recv()
+            attend(j, k)
 
     def columns_of(pieces):
         height = -(-len(pieces) // 8) * 8
@@ -251,7 +299,12 @@
             tile = jnp.where(index == i, piece, tile)
         return tile.T
 
-    for k in range(kv_local):
+    from_z = {}
+    for k in range(kv_local):
+        with jax.named_scope(f"part_wait{k}"):
+            for j in range(1, nt):
+                for copy in copies[j, k]:
+                    copy.wait_recv()
         peaks = [stat_tp[j, k, 0:1, :] for j in range(nt)]
         top = peaks[0]
         for piece in peaks[1:]:
@@ -272,18 +325,32 @@
         z_part[0, k] = joined[:sub]
         for a in range(1, nz):
             z_send[a, k] = joined[a * sub : (a + 1) * sub]
-    from_z = {}
-    for a in reversed(z_order):
-        target = {"kvb": z_back(a)}
-        from_z[a] = (
-            remote(z_stat_send, z_stat.at[a], zs_send.at[a], zs_recv.at[a], target),
-            remote(z_send.at[a], z_part.at[a], zp_send.at[a], zp_recv.at[a], target),
-        )
-    for a in z_order:
-        for copy in from_z[a]:
-            copy.wait_recv()
-
-    for k in range(kv_local):
+        for a in reversed(z_order):
+            target = {"kvb": z_back(a)}
+            from_z[a, k] = (
+                remote(
+                    z_stat_send.at[k],
+                    z_stat.at[a, k],
+                    zs_send.at[a, k],
+                    zs_recv.at[a, k],
+                    target,
+                ),
+                remote(
+                    z_send.at[a, k],
+                    z_part.at[a, k],
+                    zp_send.at[a, k],
+                    zp_recv.at[a, k],
+                    target,
+                ),
+            )
+
+    step = min(1024, width)
+    reduced = {}
+    for k in range(kv_local):
+        with jax.named_scope(f"z_wait{k}"):
+            for a in z_order:
+                for copy in from_z[a, k]:
+                    copy.wait_recv()
         spread_stat = columns_of([z_stat[a, k, i : i + 1, :] for a in range(nz) for i in range(2)])
         peaks = [spread_stat[a * sub : (a + 1) * sub, 2 * a : 2 * a + 1] for a in range(nz)]
         sums = [spread_stat[a * sub : (a + 1) * sub, 2 * a + 1 : 2 * a + 2] for a in range(nz)]
@@ -298,53 +365,61 @@
             numerator += scale * z_part[a, k].astype(jnp.float32)
         row_buf[k] = numerator / denominator
         for q in range(per_kv):
-            head = k * per_kv + q
-            lhs_buf[0:seq_rep, head * HD : (head + 1) * HD] = row_buf[
+            lhs_buf[k, 0:seq_rep, q * HD : (q + 1) * HD] = row_buf[
                 k, q * seq_rep : (q + 1) * seq_rep, :
             ]
-    attended = lhs_buf[...].astype(jnp.bfloat16)
-
-    step = min(512, width)
-    reduced = {}
-    for j in far_first + [0]:
-        weight_copies[j].wait()
-
-        def column_step(i, carry, j=j):
-            at = pl.ds(pl.multiple_of(i * step, LANES), step)
-            got = jnp.dot(attended, weight_buf[j, :, at], preferred_element_type=jnp.float32)
-            proj_send[j, :, at] = got[:seq_rep]
-            return carry
-
-        lax.fori_loop(0, width // step, column_step, 0)
-        if j > 0:
-            reduced[j] = remote(
-                proj_send.at[j],
-                proj_recv.at[j],
-                rs_send.at[j],
-                rs_recv.at[j],
-                {"tp": tp_to(j)},
-            )
-    own = pl.ds(pl.multiple_of(t * width, LANES), width)
+        attended = lhs_buf[k].astype(jnp.bfloat16)
+        with jax.named_scope(f"weight_wait{k}"):
+            for copy in weight_copies[k * pieces : (k + 1) * pieces]:
+                copy.wait()
+        for j in far_first + [0]:
+            column = tp_to(j) * width
+
+            def column_step(i, carry, j=j, k=k, column=column, attended=attended):
+                at = pl.ds(pl.multiple_of(i * step, LANES), step)
+                source = pl.ds(pl.multiple_of(column + i * step, LANES), step)
+                got = jnp.dot(
+                    attended,
+                    weight_buf[k * depth : (k + 1) * depth, source],
+                    preferred_element_type=jnp.float32,
+                )[:seq_rep]
+                if k > 0:
+                    got += proj_send[j, :, at]
+                proj_send[j, :, at] = got
+                return carry
+
+            lax.fori_loop(0, width // step, column_step, 0)
+            if j > 0 and k == kv_local - 1:
+                reduced[j] = remote(
+                    proj_send.at[j],
+                    proj_recv.at[j],
+                    rs_send.at[j],
+                    rs_recv.at[j],
+                    {"tp": tp_to(j)},
+                )
     summed = proj_send[0]
+    with jax.named_scope("sum_wait"):
+        for j in far_first:
+            reduced[j].wait_recv()
     for j in far_first:
-        reduced[j].wait_recv()
         summed += proj_recv[j]
-    stream = (residual_ref[:, own].astype(jnp.float32) + summed).astype(jnp.bfloat16)
-    stream_ref[...] = stream
+    stream = (residual_ref[...].astype(jnp.float32) + summed).astype(jnp.bfloat16)
     stream_wide = stream.astype(jnp.float32)
+    stream_ref[...] = stream_wide
     square = jnp.sum(stream_wide * stream_wide, axis=1, keepdims=True)
     ss_send[...] = jnp.broadcast_to(square, ss_send.shape)
     squares = [
         remote(ss_send, ss_recv.at[j], sq_send.at[j], sq_recv.at[j], {"tp": tp_to(j)})
         for j in far_first
     ]
-    gain = gain_ref[...].astype(jnp.float32)
-    for copy in squares:
-        copy.wait_recv()
+    gain = gain_ref[...].astype(jnp.float32).reshape(1, width)
+    with jax.named_scope("square_wait"):
+        for copy in squares:
+            copy.wait_recv()
     for j in range(1, nt):
         square += ss_recv[j][:, 0:1]
     mean_square = square * (1.0 / (width * nt))
-    normed_ref[...] = (stream_wide * lax.rsqrt(mean_square + EPSILON) * gain).astype(jnp.bfloat16)
+    factor_ref[...] = lax.rsqrt(mean_square + EPSILON) * gain
     for copy in pending:
         copy.wait_send()
 
@@ -381,17 +456,23 @@
     def body(*refs):
         kernel(nz, nt, seq_rep, local_heads, *refs)
 
-    return pl.pallas_call(
+    stream, factor = pl.pallas_call(
         body,
         out_shape=(
-            jax.ShapeDtypeStruct((seq_rep, width), bf16),
-            jax.ShapeDtypeStruct((seq_rep, width), bf16),
+            jax.ShapeDtypeStruct((seq_rep, width), f32),
+            jax.ShapeDtypeStruct((seq_rep, width), f32),
         ),
-        in_specs=[smem, smem, vmem, vmem, vmem, vmem, vmem, vmem, hbm, hbm],
+        in_specs=[smem, smem] + [hbm] * 8,
         out_specs=(vmem, vmem),
         scratch_shapes=[
+            pltpu.VMEM((1, slots), jnp.int32),
+            pltpu.VMEM((1, slots), jnp.int32),
+            pltpu.VMEM((seq_rep, width), bf16),
+            pltpu.VMEM(queries.shape, bf16),
+            pltpu.VMEM(new_kv.shape, bf16),
+            pltpu.VMEM((width,), bf16),
             pltpu.VMEM((tokens, kv_cache.shape[2]), bf16),
-            pltpu.VMEM((nt, depth, width), bf16),
+            pltpu.VMEM(out_weight.shape, bf16),
             pltpu.VMEM((rows, tokens), f32),
             pltpu.VMEM((kv_local, sub, HD), f32),
             pltpu.VMEM((kv_local, 2, sub, HD), f32),
@@ -404,25 +485,26 @@
             pltpu.VMEM((kv_local, 8, rows), f32),
             pltpu.VMEM((nz, kv_local, sub, HD), bf16),
             pltpu.VMEM((nz, kv_local, 8, rows), f32),
-            pltpu.VMEM((16, depth), f32),
+            pltpu.VMEM((kv_local, 16, depth // kv_local), f32),
             pltpu.VMEM((nt, seq_rep, width), f32),
             pltpu.VMEM((nt, seq_rep, width), f32),
             pltpu.VMEM((seq_rep, LANES), f32),
             pltpu.VMEM((nt, seq_rep, LANES), f32),
+            dma((6,)),
             dma,
-            dma((nt,)),
+            dma((kv_local * 4,)),
             dma((nz,)),
             dma((nz,)),
             dma((nz, nt)),
             dma((nz, nt)),
-            dma((nt,)),
-            dma((nt,)),
-            dma((nt,)),
-            dma((nt,)),
-            dma((nz,)),
-            dma((nz,)),
-            dma((nz,)),
-            dma((nz,)),
+            dma((nt, kv_local)),
+            dma((nt, kv_local)),
+            dma((nt, kv_local)),
+            dma((nt, kv_local)),
+            dma((nz, kv_local)),
+            dma((nz, kv_local)),
+            dma((nz, kv_local)),
+            dma((nz, kv_local)),
             dma((nt,)),
             dma((nt,)),
             dma((nt,)),
@@ -439,10 +521,11 @@
         residual,
         queries,
         new_kv,
-        norm_gain.reshape(1, width),
+        norm_gain,
         kv_cache.reshape(tokens, kv_cache.shape[2]),
         out_weight,
     )
+    return (stream.astype(bf16), (stream * factor).astype(bf16))
 
 
 def solution(mesh):

time: 39.5 us -> 36.4 us (0.922)
  local copies, waits for them, and re-layouts: 3.95 us -> 0 us
  other arithmetic: 0 us -> 1.46 us
  Pallas kernels: 33.9 us -> 33.4 us
    unnamed x2 -> x0, local copies, waits for them, and re-layouts: 2.66 us -> none
    convert_element_type x0 -> x1, other arithmetic: none -> 1.46 us  [on_device(): return (stream.astype(bf16), (stream * factor).astype(bf16))]
    reshape x1 -> x0, local copies, waits for them, and re-layouts: 1.29 us -> none  [on_device(): norm_gain.reshape(1, width)]
    pallas_call x1, Pallas kernels: 33.9 us -> 33.4 us  [on_device(): pl.pallas_call(body, out_shape=(jax.ShapeDtypeStruct((seq_rep, width), f3...]
where the time goes in v2:
time: 36.4 us; the launch traced here: 36.2 us
  Pallas kernels  33.4 us (92%)
  other arithmetic  1.46 us (4%)
  between operations  1.29 us (4%)
    pallas_call x1, Pallas kernels, on_device(): pl.pallas_call(body, out_shape=(jax.ShapeDtypeStruct((seq_rep, width), f3...  33.4 us
    convert_element_type x1, other arithmetic, on_device(): return (stream.astype(bf16), (stream * factor).astype(bf16))  1.46 us

profile of v2, /device:TPU:0, one launch (start us, length us, event | category | flops | bytes accessed | tf_op | source)
XLA Modules:
  0.0 36.2 jit_solution(5486618651560341708)
XLA Ops:
  1.3 33.4 %shard_map.113 = (f32[4,2048]{1,0:T(4,128)}, f32[4,2048]{1,0:T(4,128)}) custom-call(s32[16]{0:T(128)} %refs_0_.1, s32[1]{0:T(128)S(6)} %copy.12.refs_1_, s32[1,64]{1,0:T(1,128)} %bitcast.4, s32[1,64]{1,0:T(1,128)} %bitcast.5, bf16[4,8192]{1,0:T(4,128)(2,1)} %refs_4_.1, bf16[4,2048]{1,0:T(4,128)(2,1)} %refs_5_.1, bf16[4,2048]{1,0:T(4,128)(2,1)} %refs_6_.1, ...), custom_call_target="tpu_custom_call" | custom-call | tf_op jit(solution)/shard_map/pallas_call | solution.py:459
  34.7 1.5 %multiply_convert_fusion = (bf16[4,2048]{1,0:T(4,128)(2,1)}, bf16[4,2048]{1,0:T(4,128)(2,1)}) fusion(f32[4,2048]{1,0:T(4,128)} %get-tuple-element.4, f32[4,2048]{1,0:T(4,128)} %get-tuple-element.5), kind=kLoop, calls=%fused_computation | loop fusion | flops 24576 | bytes 98304 | tf_op jit(solution)/shard_map/convert_element_type | solution.py:528

commit v3 on v2

--- a/solution.py
+++ b/solution.py
@@ -58,6 +58,7 @@
     z_part,
     z_stat,
     lhs_buf,
+    proj_sum,
     proj_send,
     proj_recv,
     ss_send,
@@ -169,8 +170,25 @@
         )
     q_from_tp = {}
 
+    def relayed(j):
+        return fast == 2 and j > 2 and j % 2 == 1
+
+    def relay(j):
+        for a in [0] + z_order:
+            with jax.named_scope(f"q_relay_wait{j}"):
+                q_from_tp[a, j].wait_recv()
+            q_from_tp[a, j + 1] = remote(
+                q_all.at[j, a],
+                q_all.at[j + 1, a],
+                qt_send.at[a, j + 1],
+                qt_recv.at[a, j + 1],
+                {"tp": tp_to(1)},
+            )
+
     def forward(a):
         for j in far_first:
+            if relayed(j):
+                continue
             q_from_tp[a, j] = remote(
                 q_all.at[0, a],
                 q_all.at[j, a],
@@ -284,7 +302,10 @@
     arrived = set()
     for k in range(kv_local):
         for j in far_first if k == kv_local - 1 else range(1, nt):
-            if j not in arrived:
+            if j not in arrived and relayed(j + 1):
+                arrived.add(j)
+                relay(j)
+            elif j not in arrived:
                 arrived.add(j)
                 with jax.named_scope(f"q_tp_wait{j}"):
                     for a in range(nz):
@@ -344,7 +365,7 @@
                 ),
             )
 
-    step = min(1024, width)
+    step = width
     reduced = {}
     for k in range(kv_local):
         with jax.named_scope(f"z_wait{k}"):
@@ -384,8 +405,11 @@
                     preferred_element_type=jnp.float32,
                 )[:seq_rep]
                 if k > 0:
-                    got += proj_send[j, :, at]
-                proj_send[j, :, at] = got
+                    got += proj_sum[j, :, at]
+                if j > 0 and k == kv_local - 1:
+                    proj_send[j, :, at] = got.astype(jnp.bfloat16)
+                else:
+                    proj_sum[j, :, at] = got
                 return carry
 
             lax.fori_loop(0, width // step, column_step, 0)
@@ -397,12 +421,12 @@
                     rs_recv.at[j],
                     {"tp": tp_to(j)},
                 )
-    summed = proj_send[0]
+    summed = proj_sum[0]
     with jax.named_scope("sum_wait"):
         for j in far_first:
             reduced[j].wait_recv()
     for j in far_first:
-        summed += proj_recv[j]
+        summed += proj_recv[j].astype(jnp.float32)
     stream = (residual_ref[...].astype(jnp.float32) + summed).astype(jnp.bfloat16)
     stream_wide = stream.astype(jnp.float32)
     stream_ref[...] = stream_wide
@@ -487,7 +511,8 @@
             pltpu.VMEM((nz, kv_local, 8, rows), f32),
             pltpu.VMEM((kv_local, 16, depth // kv_local), f32),
             pltpu.VMEM((nt, seq_rep, width), f32),
-            pltpu.VMEM((nt, seq_rep, width), f32),
+            pltpu.VMEM((nt, seq_rep, width), bf16),
+            pltpu.VMEM((nt, seq_rep, width), bf16),
             pltpu.VMEM((seq_rep, LANES), f32),
             pltpu.VMEM((nt, seq_rep, LANES), f32),
             dma((6,)),

time: 36.4 us -> 35 us (0.962)
  Pallas kernels: 33.4 us -> 32 us
    pallas_call x1, Pallas kernels: 33.4 us -> 32 us  [on_device(): pl.pallas_call(body, out_shape=(jax.ShapeDtypeStruct((seq_rep, width), f3...]
where the time goes in v3:
time: 35 us; the launch traced here: 34.8 us
  Pallas kernels  32 us (91%)
  other arithmetic  1.46 us (4%)
  between operations  1.29 us (4%)
    pallas_call x1, Pallas kernels, on_device(): pl.pallas_call(body, out_shape=(jax.ShapeDtypeStruct((seq_rep, width), f3...  32 us
    convert_element_type x1, other arithmetic, on_device(): return (stream.astype(bf16), (stream * factor).astype(bf16))  1.46 us

profile of v3, /device:TPU:0, one launch (start us, length us, event | category | flops | bytes accessed | tf_op | source)
XLA Modules:
  0.0 34.8 jit_solution(3162168703374730989)
XLA Ops:
  1.3 32.0 %shard_map.113 = (f32[4,2048]{1,0:T(4,128)}, f32[4,2048]{1,0:T(4,128)}) custom-call(s32[16]{0:T(128)} %refs_0_.1, s32[1]{0:T(128)S(6)} %copy.12.refs_1_, s32[1,64]{1,0:T(1,128)} %bitcast.4, s32[1,64]{1,0:T(1,128)} %bitcast.5, bf16[4,8192]{1,0:T(4,128)(2,1)} %refs_4_.1, bf16[4,2048]{1,0:T(4,128)(2,1)} %refs_5_.1, bf16[4,2048]{1,0:T(4,128)(2,1)} %refs_6_.1, ...), custom_call_target="tpu_custom_call" | custom-call | tf_op jit(solution)/shard_map/pallas_call | solution.py:483
  33.3 1.5 %multiply_convert_fusion = (bf16[4,2048]{1,0:T(4,128)(2,1)}, bf16[4,2048]{1,0:T(4,128)(2,1)}) fusion(f32[4,2048]{1,0:T(4,128)} %get-tuple-element.4, f32[4,2048]{1,0:T(4,128)} %get-tuple-element.5), kind=kLoop, calls=%fused_computation | loop fusion | flops 24576 | bytes 98304 | tf_op jit(solution)/shard_map/convert_element_type | solution.py:553
